TPU v7x, 32 devices: a whole 2x2x4 slice. The times are simulated.
32 devices in a mesh: dp: 8 (over z, y), rep: 4 (over x, core).
Axes of the slice: x: 2, y: 2, z: 4, core: 2. Of those that a mesh axis runs over, the one named last changes fastest.
Arguments:
- enc: bfloat16 [64, 48, 640], P(('dp', 'rep')), may hold values from -6 to 6
- pred: bfloat16 [64, 17, 640], P(('dp', 'rep')), may hold values from -6 to 6
- labels: int32 [64, 16], P(('dp', 'rep')), may hold values from 1 to 4095
- frame_len: int32 [64], P(('dp', 'rep')), may hold values from 24 to 48, as said below
- label_len: int32 [64], P(('dp', 'rep')), may hold values from 1 to 16, as said below
- w_enc: bfloat16 [640, 640], replicated, may hold values from -0.25 to 0.25
- w_pred: bfloat16 [640, 640], replicated, may hold values from -0.25 to 0.25
- b_joint: bfloat16 [640], replicated, may hold values from -3 to 3
- w_out: bfloat16 [640, 4096], replicated, may hold values from -0.69921875 to 0.69921875
- b_out: bfloat16 [4096], replicated, may hold values from -5 to 5
Outputs:
- step_enc: float32 [640, 640], replicated
- step_pred: float32 [640, 640], replicated
- step_out: float32 [640, 4096], replicated
- step_bias_out: float32 [4096], replicated
- step_bias_joint: float32 [640], replicated
- mean_loss: float32 [], replicated
Inputs may be any that keep to these rules, and one draw needn't show every extreme that they name: `frame_len`: the last utterance has all 48 frames. `label_len`: the last utterance has all 16 labels.
All inputs are finite; a program needn't handle non-finite values.
Results may differ from a plain program's by a relative error of at most 0.0055.
Values sent between devices are 32-bit elements; how exact they have to be, the bound alone decides.
No kernel may reach another device: no remote copies, remote signals or barrier semaphores. Data moves between devices by JAX's collectives and lax.ppermute only.
A program may use at most 256 MiB of HBM per device.

v0:
```python
import jax
import jax.numpy as jnp
from jax import lax
from jax.sharding import PartitionSpec as P

NEG = -1e30
EPS = 1e-06


def diagonal_index(num_frames, count_labels):
    diagonals = jnp.arange(num_frames + count_labels - 1, dtype=jnp.int32)
    positions = jnp.arange(count_labels, dtype=jnp.int32)
    return diagonals[:, None] - positions[None, :]


def skewed(grid):
    utterances, num_frames, count_labels = grid.shape
    positions = jnp.arange(count_labels, dtype=jnp.int32)
    frame_index = diagonal_index(num_frames, count_labels)
    inside = (frame_index >= 0) & (frame_index < num_frames)
    picked = grid[:, jnp.clip(frame_index, 0, num_frames - 1), positions[None, :]]
    picked = jnp.where(inside[None, :, :], picked, NEG)
    return jnp.transpose(picked, (1, 0, 2))


def unskewed(diag_grid, num_frames):
    count_labels = diag_grid.shape[2]
    by_utterance = jnp.transpose(diag_grid, (1, 0, 2))
    frame_ids = jnp.arange(num_frames, dtype=jnp.int32)
    positions = jnp.arange(count_labels, dtype=jnp.int32)
    return by_utterance[:, frame_ids[:, None] + positions[None, :], positions[None, :]]


def lattice(blank, emit, frame_len, label_len):
    utterances, num_frames, count_labels = blank.shape
    positions = jnp.arange(count_labels, dtype=jnp.int32)
    frame_index = diagonal_index(num_frames, count_labels)
    blank_diag = skewed(blank)
    emit_diag = skewed(emit)
    neg_block = jnp.full((1, utterances, count_labels), NEG, jnp.float32)
    neg_col = jnp.full((utterances, 1), NEG, jnp.float32)
    neg_grid = jnp.full((utterances, count_labels), NEG, jnp.float32)
    frame_count = frame_len[:, None]
    label_count = label_len[:, None]
    terminal = jnp.where(positions[None, :] == label_count, 0.0, NEG).astype(jnp.float32)
    first_diag = jnp.broadcast_to(
        jnp.where(positions == 0, 0.0, NEG).astype(jnp.float32)[None, :], (utterances, count_labels)
    )
    blank_prev = jnp.concatenate([neg_block, blank_diag[:-1]], axis=0)
    emit_prev = jnp.concatenate([neg_block, emit_diag[:-1]], axis=0)
    steps_total = frame_index.shape[0]
    step_ids = jnp.arange(steps_total, dtype=jnp.int32)

    def both_ways(carry, inputs):
        alpha_prev, beta_next = carry
        step_id, blank_fwd, emit_fwd, frames_fwd, blank_back, emit_back, frames_back = inputs
        top_term = alpha_prev + blank_fwd
        left_term = jnp.concatenate([neg_col, (alpha_prev + emit_fwd)[:, :-1]], axis=1)
        alpha_cell = jnp.logaddexp(top_term, left_term)
        inside = (frames_fwd >= 0) & (frames_fwd < num_frames)
        alpha_cell = jnp.where(inside[None, :], alpha_cell, NEG)
        alpha_cell = jnp.where(step_id == 0, first_diag, alpha_cell)
        frames_row = frames_back[None, :]
        below = jnp.where(
            frames_row == frame_count - 1,
            terminal,
            jnp.where(frames_row >= frame_count, neg_grid, beta_next),
        )
        right_term = jnp.concatenate([beta_next[:, 1:], neg_col], axis=1)
        beta_cell = jnp.logaddexp(below + blank_back, right_term + emit_back)
        live = (positions[None, :] <= label_count) & (frames_row < frame_count) & (frames_row >= 0)
        beta_cell = jnp.where(live, beta_cell, NEG)
        return ((alpha_cell, beta_cell), (alpha_cell, beta_cell, below))

    inputs = (
        step_ids,
        blank_prev,
        emit_prev,
        frame_index,
        jnp.flip(blank_diag, 0),
        jnp.flip(emit_diag, 0),
        jnp.flip(frame_index, 0),
    )
    unused_last, (alpha_diag, beta_rev, below_rev) = lax.scan(
        both_ways, (first_diag, neg_grid), inputs
    )
    alpha = unskewed(alpha_diag, num_frames)
    beta = unskewed(jnp.flip(beta_rev, 0), num_frames)
    below = unskewed(jnp.flip(below_rev, 0), num_frames)
    return (alpha, beta, below)


def joint_forward(enc_row, pred_row, label_row, w_enc, w_pred, b_joint, w_out, b_out):
    num_frames = enc_row.shape[0]
    count_labels = pred_row.shape[0]
    joint_width = w_enc.shape[1]
    vocab_size = w_out.shape[1]
    enc_proj = jnp.dot(enc_row, w_enc, preferred_element_type=jnp.float32)
    pred_proj = jnp.dot(pred_row, w_pred, preferred_element_type=jnp.float32) + b_joint.astype(
        jnp.float32
    )
    hidden = jnp.tanh(enc_proj[:, None, :] + pred_proj[None, :, :]).astype(jnp.bfloat16)
    hidden = lax.optimization_barrier(hidden.reshape(num_frames * count_labels, joint_width))
    logits = jnp.dot(hidden, w_out, preferred_element_type=jnp.float32) + b_out.astype(jnp.float32)
    log_probs = jax.nn.log_softmax(logits, axis=-1)
    targets = jnp.concatenate([label_row, jnp.ones((1,), jnp.int32)])
    target_cols = jnp.tile(targets, num_frames)
    vocab_pos = jnp.arange(vocab_size, dtype=jnp.int32)
    is_target = vocab_pos[None, :] == target_cols[:, None]
    emit = jnp.sum(jnp.where(is_target, log_probs, 0.0), axis=1).reshape(num_frames, count_labels)
    blank = log_probs[:, 0].reshape(num_frames, count_labels)
    return (hidden, log_probs, blank, emit)


def joint_backward(
    enc_row, pred_row, label_row, hidden, log_probs, blank, emit, alpha, beta, below, w_out
):
    num_frames = enc_row.shape[0]
    count_labels = pred_row.shape[0]
    joint_width = hidden.shape[1]
    vocab_size = w_out.shape[1]
    targets = jnp.concatenate([label_row, jnp.ones((1,), jnp.int32)])
    target_cols = jnp.tile(targets, num_frames)
    vocab_pos = jnp.arange(vocab_size, dtype=jnp.int32)
    is_target = vocab_pos[None, :] == target_cols[:, None]
    log_total = beta[0, 0]
    right = jnp.concatenate([beta[:, 1:], jnp.full((num_frames, 1), NEG, jnp.float32)], axis=1)
    blank_occ = jnp.exp(alpha + blank + below - log_total).reshape(-1)
    emit_occ = jnp.exp(alpha + emit + right - log_total).reshape(-1)
    probs = jnp.exp(log_probs)
    grad_logits = probs * (blank_occ + emit_occ)[:, None]
    grad_logits = grad_logits - jnp.where(vocab_pos[None, :] == 0, blank_occ[:, None], 0.0)
    grad_logits = grad_logits - jnp.where(is_target, emit_occ[:, None], 0.0)
    grad_logits = lax.optimization_barrier(grad_logits.astype(jnp.bfloat16))
    grad_out = lax.dot_general(
        hidden, grad_logits, (((0,), (0,)), ((), ())), preferred_element_type=jnp.float32
    )
    grad_bias_out = jnp.sum(grad_logits.astype(jnp.float32), axis=0)
    grad_hidden = lax.dot_general(
        grad_logits, w_out, (((1,), (1,)), ((), ())), preferred_element_type=jnp.float32
    )
    hidden_wide = hidden.astype(jnp.float32)
    grad_pre = (grad_hidden * (1.0 - hidden_wide * hidden_wide)).reshape(
        num_frames, count_labels, joint_width
    )
    grad_enc_proj = lax.optimization_barrier(jnp.sum(grad_pre, axis=1).astype(jnp.bfloat16))
    grad_pred_proj = lax.optimization_barrier(jnp.sum(grad_pre, axis=0).astype(jnp.bfloat16))
    grad_enc = lax.dot_general(
        enc_row, grad_enc_proj, (((0,), (0,)), ((), ())), preferred_element_type=jnp.float32
    )
    grad_pred = lax.dot_general(
        pred_row, grad_pred_proj, (((0,), (0,)), ((), ())), preferred_element_type=jnp.float32
    )
    grad_bias_joint = jnp.sum(grad_pred_proj.astype(jnp.float32), axis=0)
    return (-log_total, (grad_enc, grad_pred, grad_out, grad_bias_out, grad_bias_joint))


def local_sums(enc, pred, labels, frame_len, label_len, w_enc, w_pred, b_joint, w_out, b_out):

    def forward_one(unused_carry, inputs):
        enc_row, pred_row, label_row = inputs
        return (
            None,
            joint_forward(enc_row, pred_row, label_row, w_enc, w_pred, b_joint, w_out, b_out),
        )

    unused_none, (hidden, log_probs, blank, emit) = lax.scan(forward_one, None, (enc, pred, labels))
    alpha, beta, below = lattice(blank, emit, frame_len, label_len)
    initial = (
        jnp.zeros(w_enc.shape, jnp.float32),
        jnp.zeros(w_pred.shape, jnp.float32),
        jnp.zeros(w_out.shape, jnp.float32),
        jnp.zeros(b_out.shape, jnp.float32),
        jnp.zeros(b_joint.shape, jnp.float32),
    )

    def backward_one(carry, inputs):
        loss_sum, grad_sums = carry
        loss_one, grads_one = joint_backward(*inputs, w_out)
        added = tuple((total + term for total, term in zip(grad_sums, grads_one)))
        return ((loss_sum + loss_one, added), None)

    (loss_sum, grads), unused_ys = lax.scan(
        backward_one,
        (jnp.float32(0.0), initial),
        (enc, pred, labels, hidden, log_probs, blank, emit, alpha, beta, below),
    )
    return (loss_sum, grads)


def squares(items):
    total_sq = jnp.float32(0.0)
    for item in items:
        total_sq = total_sq + jnp.sum(item * item)
    return total_sq


def per_device(enc, pred, labels, frame_len, label_len, w_enc, w_pred, b_joint, w_out, b_out):
    loss_local, grads = local_sums(
        enc, pred, labels, frame_len, label_len, w_enc, w_pred, b_joint, w_out, b_out
    )
    count_local = jnp.sum(label_len).astype(jnp.float32)
    param_count = jnp.float32(w_enc.size + w_pred.size + w_out.size + b_out.size + b_joint.size)
    loss_total, label_total = lax.psum((loss_local, count_local), ("dp", "rep"))
    summed = lax.psum((grads[0], grads[1], grads[2], grads[3], grads[4]), ("dp", "rep"))
    scale = lax.rsqrt(squares(summed) / param_count + EPS)
    result = tuple((item * scale for item in summed))
    return (result[0], result[1], result[2], result[3], result[4], loss_total / label_total)


def solution(mesh):
    in_specs = (
        P(("dp", "rep"), None, None),
        P(("dp", "rep"), None, None),
        P(("dp", "rep"), None),
        P(("dp", "rep")),
        P(("dp", "rep")),
        P(),
        P(),
        P(),
        P(),
        P(),
    )
    out_specs = (P(), P(), P(), P(), P(), P())
    return jax.shard_map(
        per_device, mesh=mesh, in_specs=in_specs, out_specs=out_specs, check_vma=False
    )
```

profile of v0, /device:TPU:0, one launch (start us, length us, event | category | flops | bytes accessed | tf_op | source)
XLA Modules:
  0.0 639.8 jit_solution(4801691328892887368)
XLA Ops:
  11.1 88.6 %while.58 = (s32[]{:T(128)}, bf16[2,816,640]{2,1,0:T(8,128)(2,1)}, f32[2,816,4096]{2,1,0:T(8,128)}, f32[2,48,17]{2,1,0:T(8,128)S(1)}, f32[2,48,17]{2,1,0:T(8,128...) while((s32[]{:T(128)}, bf16[2,816,640]{2,1,0:T(8,128)(2,1)}, ...), condition=%wide.region_4.5_spmd, body=%wide.region_0.4_spmd.sunk | while | flops 4369261056 | bytes 147507888 | solution.py:167
  11.9 1.4 convolution_add_fusion.2
  13.3 1.4 fusion.76
  16.4 7.5 %add_reduce_fusion.2 = (f32[816]{0:T(1024)S(1)}, f32[816,4096]{1,0:T(8,128)S(1)}) fusion(f32[4096]{0:T(1024)S(1)} %convert_element_type.65, bf16[816,640]{1,0:T(8,128)(2,1)S(1)} %convert_element_type.64, bf16[640,4096]{1,0:T(8,128)(2,1)} %get-tuple-element.1143), kind=kOutput, calls=%fused_computation.66.clone.1 | convolution fusion | flops 4284873984 | bytes 19676352 | tf_op jit(solution)/shard_map/while/body/eval_jaxpr/dot_general | solution.py:104
  23.9 2.3 exponential_reduce_fusion.2
  26.2 2.5 copy-done.1
  28.9 12.7 %select_reduce_fusion.2 = (f32[816]{0:T(1024)S(1)}, f32[816,4096]{1,0:T(8,128)}) fusion(s32[816]{0:T(1024)S(1)} %eq.178, f32[816]{0:T(1024)S(1)} %log.11, f32[816]{0:T(1024)S(1)} %get-tuple-element.1053, f32[816,4096]{1,0:T(8,128)} %copy-done.1, f32[4096]{0:T(1024)S(1)} %convert_element_type.65), kind=kLoop, calls=%fused_computation.62.clone.1 | loop fusion | flops 20053200 | bytes 26768128 | tf_op jit(solution)/shard_map/while/body/eval_jaxpr/reduce_sum | solution.py:110
  41.6 1.2 slice_reduce_fusion.2
  43.1 11.3 %bitcast_dynamic-update-slice_fusion.5 = f32[2,816,4096]{2,1,0:T(8,128)} fusion(f32[2,816,4096]{2,1,0:T(8,128)} %get-tuple-element.1120, s32[]{:T(128)} %get-tuple-element.1118, f32[816,4096]{1,0:T(8,128)} %get-tuple-element.1054), kind=kLoop, calls=%fused_computation.61.clone.1 | loop fusion | bytes 26739200 | tf_op jit(solution)/shard_map/while/body/jit(dynamic_update_index_in_dim)/dynamic_update_slice | solution.py:167
  54.4 1.1 bitcast_dynamic-update-slice_fusion.4
  56.1 1.4 convolution_add_fusion.2
  57.5 1.4 fusion.76
  60.6 7.5 %add_reduce_fusion.2 = (f32[816]{0:T(1024)S(1)}, f32[816,4096]{1,0:T(8,128)S(1)}) fusion(f32[4096]{0:T(1024)S(1)} %convert_element_type.65, bf16[816,640]{1,0:T(8,128)(2,1)S(1)} %convert_element_type.64, bf16[640,4096]{1,0:T(8,128)(2,1)} %get-tuple-element.1143), kind=kOutput, calls=%fused_computation.66.clone.1 | convolution fusion | flops 4284873984 | bytes 19676352 | tf_op jit(solution)/shard_map/while/body/eval_jaxpr/dot_general | solution.py:104
  68.1 2.3 exponential_reduce_fusion.2
  70.5 2.5 copy-done.1
  73.2 12.7 %select_reduce_fusion.2 = (f32[816]{0:T(1024)S(1)}, f32[816,4096]{1,0:T(8,128)}) fusion(s32[816]{0:T(1024)S(1)} %eq.178, f32[816]{0:T(1024)S(1)} %log.11, f32[816]{0:T(1024)S(1)} %get-tuple-element.1053, f32[816,4096]{1,0:T(8,128)} %copy-done.1, f32[4096]{0:T(1024)S(1)} %convert_element_type.65), kind=kLoop, calls=%fused_computation.62.clone.1 | loop fusion | flops 20053200 | bytes 26768128 | tf_op jit(solution)/shard_map/while/body/eval_jaxpr/reduce_sum | solution.py:110
  85.9 1.2 slice_reduce_fusion.2
  87.3 11.3 %bitcast_dynamic-update-slice_fusion.5 = f32[2,816,4096]{2,1,0:T(8,128)} fusion(f32[2,816,4096]{2,1,0:T(8,128)} %get-tuple-element.1120, s32[]{:T(128)} %get-tuple-element.1118, f32[816,4096]{1,0:T(8,128)} %get-tuple-element.1054), kind=kLoop, calls=%fused_computation.61.clone.1 | loop fusion | bytes 26739200 | tf_op jit(solution)/shard_map/while/body/jit(dynamic_update_index_in_dim)/dynamic_update_slice | solution.py:167
  98.6 1.1 bitcast_dynamic-update-slice_fusion.4
  100.8 12.3 %gather_fusion = f32[1088,2]{1,0:T(8,128)S(1)} fusion(f32[2,48,17]{0,1,2:T(8,128)S(1)} %copy.55, s32[1088]{0:T(1024)S(1)} %reshape.180), kind=kCustom, calls=%fused_computation | custom fusion | bytes 26112 | tf_op jit(solution)/shard_map/gather | solution.py:21
  113.6 12.1 %gather_fusion.1 = f32[1088,2]{1,0:T(8,128)S(1)} fusion(f32[2,48,17]{0,1,2:T(8,128)S(1)} %copy.57, s32[1088]{0:T(1024)S(1)} %reshape.180), kind=kCustom, calls=%fused_computation.1 | custom fusion | bytes 26112 | tf_op jit(solution)/shard_map/gather | solution.py:21
  126.3 106.5 %while.59 = (s32[]{:T(128)}, f32[2,17]{1,0:T(2,128)S(1)}, f32[2,17]{1,0:T(2,128)S(1)}, f32[64,2,17]{2,1,0:T(2,128)S(1)}, f32[64,2,17]{2,1,0:T(2,128)S(1)}, /*ind...) while((s32[]{:T(128)}, f32[2,17]{1,0:T(2,128)S(1)}, ...), condition=%wide.region_6.7_spmd.clone, body=%wide.region_5.6_spmd.clone.sunk | while | flops 1434 | bytes 22799 | solution.py:84
  233.9 9.8 %gather_fusion.2 = f32[816,2]{1,0:T(8,128)S(1)} fusion(f32[2,64,17]{0,1,2:T(8,128)S(1)} %bitcast.183, s32[816]{0:T(1024)S(1)} %reshape.192), kind=kCustom, calls=%fused_computation.2 | custom fusion | bytes 19584 | tf_op jit(solution)/shard_map/gather | solution.py:31
  245.2 10.0 %gather_fusion.4 = f32[816,2]{1,0:T(8,128)S(1)} fusion(f32[2,64,17]{0,1,2:T(8,128)S(1)} %bitcast.185, s32[816]{0:T(1024)S(1)} %reshape.192), kind=kCustom, calls=%fused_computation.4 | custom fusion | bytes 19584 | tf_op jit(solution)/shard_map/gather | solution.py:31
  256.3 9.8 %gather_fusion.3 = f32[816,2]{1,0:T(8,128)S(1)} fusion(f32[2,64,17]{0,1,2:T(8,128)S(1)} %bitcast.184, s32[816]{0:T(1024)S(1)} %reshape.192), kind=kCustom, calls=%fused_computation.3 | custom fusion | bytes 19584 | tf_op jit(solution)/shard_map/gather | solution.py:31
  266.5 91.0 %while.60 = (s32[]{:T(128)}, f32[]{:T(128)}, f32[640,640]{1,0:T(8,128)}, f32[640,640]{1,0:T(8,128)}, f32[640,4096]{1,0:T(8,128)}, /*index=5*/f32[4096]{0:T(1024)...) while((s32[]{:T(128)}, f32[]{:T(128)}, ...), condition=%wide.region_12.13_spmd.clone, body=%wide.region_7.12_spmd.clone.sunk | while | flops 8649718784 | bytes 146314000 | solution.py:183
  269.0 11.2 %fusion.89 = bf16[816,4096]{1,0:T(8,128)(2,1)} fusion(f32[2,816,4096]{2,1,0:T(8,128)} %get-tuple-element.1259, s32[]{:T(128)} %get-tuple-element.1229, f32[816]{0:T(1024)S(1)} %reshape.215, s32[816]{0:T(1024)S(1)} %eq.189, f32[816]{0:T(1024)S(1)} %exp.63, f32[816]{0:T(1024)S(1)} %add.404, pred[4096]{0:T(1024)(128)(4,1)S(1)} %iota_compare_fusion.4), kind=kLoop, calls=%fused_computation.33.clone.1 | loop fusion | flops 23396352 | bytes 20071172 | tf_op jit(solution)/shard_map/while/body/eval_jaxpr/convert_element_type | solution.py:134
  280.2 10.6 %select_add_fusion.12 = f32[640,4096]{1,0:T(8,128)} fusion(f32[640,4096]{1,0:T(8,128)} %get-tuple-element.1233, bf16[816,4096]{1,0:T(8,128)(2,1)} %fusion.89, pred[]{:T(512)S(6)} %compare.12, bf16[2,816,640]{2,1,0:T(8,128)(2,1)} %get-tuple-element.1266, s32[]{:T(128)} %get-tuple-element.1229), kind=kOutput, calls=%fused_computation.36.clone.1 | convolution fusion | flops 4283432960 | bytes 28701184 | tf_op jit(solution)/shard_map/while/body/eval_jaxpr/dot_general | solution.py:135
  290.8 8.1 %subtract_multiply_fusion.2 = f32[816,640]{1,0:T(8,128)} fusion(bf16[816,4096]{1,0:T(8,128)(2,1)S(1)} %copy-done, bf16[640,4096]{1,0:T(8,128)(2,1)S(1)} %bitcast.202, bf16[2,816,640]{2,1,0:T(8,128)(2,1)} %get-tuple-element.1266, s32[]{:T(128)} %get-tuple-element.1229), kind=kOutput, calls=%fused_computation.37.clone.1 | convolution fusion | flops 4280279040 | bytes 15060996 | tf_op jit(solution)/shard_map/while/body/eval_jaxpr/dot_general | solution.py:139
  299.0 3.1 reshape.216
  302.1 2.5 fusion.90
  304.6 1.6 select_add_fusion.11
  306.2 1.6 select_add_fusion.10
  307.8 1.1 convert_reduce_fusion.4
  312.2 11.2 %fusion.89 = bf16[816,4096]{1,0:T(8,128)(2,1)} fusion(f32[2,816,4096]{2,1,0:T(8,128)} %get-tuple-element.1259, s32[]{:T(128)} %get-tuple-element.1229, f32[816]{0:T(1024)S(1)} %reshape.215, s32[816]{0:T(1024)S(1)} %eq.189, f32[816]{0:T(1024)S(1)} %exp.63, f32[816]{0:T(1024)S(1)} %add.404, pred[4096]{0:T(1024)(128)(4,1)S(1)} %iota_compare_fusion.4), kind=kLoop, calls=%fused_computation.33.clone.1 | loop fusion | flops 23396352 | bytes 20071172 | tf_op jit(solution)/shard_map/while/body/eval_jaxpr/convert_element_type | solution.py:134
  323.4 12.1 %select_add_fusion.12 = f32[640,4096]{1,0:T(8,128)} fusion(f32[640,4096]{1,0:T(8,128)} %get-tuple-element.1233, bf16[816,4096]{1,0:T(8,128)(2,1)} %fusion.89, pred[]{:T(512)S(6)} %compare.12, bf16[2,816,640]{2,1,0:T(8,128)(2,1)} %get-tuple-element.1266, s32[]{:T(128)} %get-tuple-element.1229), kind=kOutput, calls=%fused_computation.36.clone.1 | convolution fusion | flops 4283432960 | bytes 28701184 | tf_op jit(solution)/shard_map/while/body/eval_jaxpr/dot_general | solution.py:135
  335.8 8.1 %subtract_multiply_fusion.2 = f32[816,640]{1,0:T(8,128)} fusion(bf16[816,4096]{1,0:T(8,128)(2,1)S(1)} %copy-done, bf16[640,4096]{1,0:T(8,128)(2,1)S(1)} %bitcast.202, bf16[2,816,640]{2,1,0:T(8,128)(2,1)} %get-tuple-element.1266, s32[]{:T(128)} %get-tuple-element.1229), kind=kOutput, calls=%fused_computation.37.clone.1 | convolution fusion | flops 4280279040 | bytes 15060996 | tf_op jit(solution)/shard_map/while/body/eval_jaxpr/dot_general | solution.py:139
  343.9 3.1 reshape.216
  347.0 2.5 fusion.90
  349.5 3.0 select_add_fusion.11
  352.6 3.0 select_add_fusion.10
  355.6 1.1 convert_reduce_fusion.4
  359.4 44.8 %all-reduce.5 = (f32[4096]{0:T(1024)S(1)}, f32[640]{0:T(1024)S(1)}, f32[]{:T(128)}, f32[]{:T(128)}) all-reduce(f32[4096]{0:T(1024)S(1)} %get-tuple-element.406, f32[640]{0:T(1024)S(1)} %get-tuple-element.407, f32[]{:T(128)} %get-tuple-element.408, f32[]{:T(128)S(6)} %convert_element_type.42), channel_id=1, replica_groups=mesh['dp'=8,'rep'=4] {'dp','rep'}, use_global_device_ids=true, to_apply=%region_19.20 | all-reduce | flops 4738 | bytes 37904 | tf_op jit(solution)/shard_map/psum | solution.py:205
  406.7 199.6 %all-reduce.9.cloned.1.call-done = (f32[640,640]{1,0:T(8,128)}, f32[640,640]{1,0:T(8,128)}, f32[640,4096]{1,0:T(8,128)}) async-done(((f32[640,640]{1,0:T(8,128)}, f32[640,640]{1,0:T(8,128)}, f32[640,4096]{1,0:T(8,128)}), (f32[640,640]{1,0:T(8,128)}, f32[640,640]{1,0:T(8,128)}, f32[640,4096]{1,0:T(8,128)})) %all-reduce.9.cloned.1.call-update) | async-done | bytes 13762576 | tf_op jit(solution)/shard_map/psum | solution.py:205
  606.3 7.4 %multiply_reduce_fusion = f32[]{:T(128)} fusion(f32[640,4096]{1,0:T(8,128)} %get-tuple-element.759), kind=kLoop, calls=%fused_computation.83 | loop fusion | flops 5242879 | bytes 10485764 | tf_op jit(solution)/shard_map/reduce_sum | solution.py:194
  619.2 9.7 %broadcast_multiply_fusion = f32[640,4096]{1,0:T(8,128)} fusion(f32[640,4096]{1,0:T(8,128)} %get-tuple-element.759, f32[]{:T(128)S(6)} %rsqrt.3), kind=kLoop, calls=%fused_computation.84 | loop fusion | flops 2621440 | bytes 20971524 | tf_op jit(solution)/shard_map/mul | solution.py:207
  628.8 1.3 broadcast_multiply_fusion.1
  630.1 1.3 broadcast_multiply_fusion.2
  (949 shorter events, 85.9 us)
Async XLA Ops:
  7.2 599.1 %all-reduce.9.cloned.1.call-start = ((), (), s32[]{:S(2)}) async-start(), calls=%async_computation | async-start | bytes 27525120 | tf_op jit(solution)/shard_map/psum | solution.py:205
  11.0 89.7 %copy-start.5 = (s32[64,17,1]{1,0,2:T(8,128)S(1)}, s32[64,17,1]{1,0,2:T(8,128)}, u32[]{:S(2)}) copy-start(s32[64,17,1]{1,0,2:T(8,128)} %fusion.34) | copy-start | bytes 13060
  11.0 115.0 %copy-start.14 = (pred[64,17]{1,0:T(8,128)(4,1)S(1)}, pred[64,17]{1,0:T(8,128)(4,1)}, u32[]{:S(2)}) copy-start(pred[64,17]{1,0:T(8,128)(4,1)} %compare_and_fusion) | copy-start | bytes 3268
  11.0 115.1 %copy-start.6 = (s32[64,17]{1,0:T(8,128)S(1)}, s32[64,17]{1,0:T(8,128)}, u32[]{:S(2)}) copy-start(s32[64,17]{1,0:T(8,128)} %iota_subtract_fusion) | copy-start | bytes 13060
  11.0 115.2 %copy-start.16 = (f32[17]{0:T(128)S(1)}, f32[17]{0:T(128)}, u32[]{:S(2)}) copy-start(f32[17]{0:T(128)} %compare_select_fusion.7) | copy-start | bytes 208
  11.1 115.2 %copy-start.7 = (s32[2]{0:T(128)S(1)}, s32[2]{0:T(128)}, u32[]{:S(2)}) copy-start(s32[2]{0:T(128)} %param.20) | copy-start | bytes 28
  11.1 115.2 %copy-start.10 = (f32[64,2,17]{2,1,0:T(2,128)S(1)}, f32[64,2,17]{2,1,0:T(2,128)}, u32[]{:S(2)}) copy-start(f32[64,2,17]{2,1,0:T(2,128)} %custom-call.20) | copy-start | bytes 26116
  11.1 115.2 %copy-start.11 = (f32[64,2,17]{2,1,0:T(2,128)S(1)}, f32[64,2,17]{2,1,0:T(2,128)}, u32[]{:S(2)}) copy-start(f32[64,2,17]{2,1,0:T(2,128)} %custom-call.21) | copy-start | bytes 26116
  11.1 115.2 %copy-start.12 = (f32[64,2,17]{2,1,0:T(2,128)S(1)}, f32[64,2,17]{2,1,0:T(2,128)}, u32[]{:S(2)}) copy-start(f32[64,2,17]{2,1,0:T(2,128)} %custom-call.22) | copy-start | bytes 26116
  11.1 115.2 %copy-start.13 = (s32[2]{0:T(128)S(1)}, s32[2]{0:T(128)}, u32[]{:S(2)}) copy-start(s32[2]{0:T(128)} %param.19) | copy-start | bytes 28
  11.1 115.2 %copy-start.15 = (f32[2,17]{1,0:T(2,128)S(1)}, f32[2,17]{1,0:T(2,128)}, u32[]{:S(2)}) copy-start(f32[2,17]{1,0:T(2,128)} %custom-call.10) | copy-start | bytes 412
  23.9 4.8 copy-start.1
  23.9 4.8 copy-start.17
  68.1 4.8 copy-start.1
  68.1 4.8 copy-start.17
  99.7 134.1 %copy-start.9 = (s32[48,17,1]{1,0,2:T(8,128)S(1)}, s32[48,17,1]{1,0,2:T(8,128)}, u32[]{:S(2)}) copy-start(s32[48,17,1]{1,0,2:T(8,128)} %fusion.37) | copy-start | bytes 9796
  113.2 153.3 %copy-start.4 = (bf16[2,48,640]{2,1,0:T(8,128)(2,1)S(1)}, bf16[2,48,640]{2,1,0:T(8,128)(2,1)}, u32[]{:S(2)}) copy-start(bf16[2,48,640]{2,1,0:T(8,128)(2,1)} %get-tuple-element.1284) | copy-start | bytes 368644
  113.2 153.3 %copy-start.18 = (s32[2,16]{1,0:T(2,128)S(1)}, s32[2,16]{1,0:T(2,128)}, u32[]{:S(2)}) copy-start(s32[2,16]{1,0:T(2,128)} %get-tuple-element.1288) | copy-start | bytes 388
  269.0 21.8 %slice-start.2 = ((s8[5242880]{0:T(1024)(128)(4,1)}), s8[1048576]{0:T(1024)(128)(4,1)S(1)}, s32[]{:S(2)}) async-start(s8[5242880]{0:T(1024)(128)(4,1)} %bitcast.201), calls=%async_computation.3 | async-start | bytes 2097152 | tf_op jit(solution)/shard_map/while
  280.2 10.6 %copy-start = (bf16[816,4096]{1,0:T(8,128)(2,1)S(1)}, bf16[816,4096]{1,0:T(8,128)(2,1)}, u32[]{:S(2)}) copy-start(bf16[816,4096]{1,0:T(8,128)(2,1)} %fusion.89) | copy-start | bytes 20054020 | tf_op jit(solution)/shard_map/while
  280.2 10.6 %slice-start.3 = ((s8[5242880]{0:T(1024)(128)(4,1)}), s8[4194304]{0:T(1024)(128)(4,1)S(1)}, s32[]{:S(2)}) async-start(s8[5242880]{0:T(1024)(128)(4,1)} %bitcast.201), calls=%async_computation.4 | async-start | bytes 8388608 | tf_op jit(solution)/shard_map/while
  299.0 8.8 %slice-start = ((s8[6684672]{0:T(1024)(128)(4,1)}), s8[2490368]{0:T(1024)(128)(4,1)S(1)}, s32[]{:S(2)}) async-start(s8[6684672]{0:T(1024)(128)(4,1)} %bitcast.181), calls=%async_computation.1 | async-start | bytes 4980736 | tf_op jit(solution)/shard_map/while
  302.1 5.7 slice-start.1
  312.2 23.3 %slice-start.2 = ((s8[5242880]{0:T(1024)(128)(4,1)}), s8[1048576]{0:T(1024)(128)(4,1)S(1)}, s32[]{:S(2)}) async-start(s8[5242880]{0:T(1024)(128)(4,1)} %bitcast.201), calls=%async_computation.3 | async-start | bytes 2097152 | tf_op jit(solution)/shard_map/while
  323.4 12.1 %copy-start = (bf16[816,4096]{1,0:T(8,128)(2,1)S(1)}, bf16[816,4096]{1,0:T(8,128)(2,1)}, u32[]{:S(2)}) copy-start(bf16[816,4096]{1,0:T(8,128)(2,1)} %fusion.89) | copy-start | bytes 20054020 | tf_op jit(solution)/shard_map/while
  323.4 12.4 %slice-start.3 = ((s8[5242880]{0:T(1024)(128)(4,1)}), s8[4194304]{0:T(1024)(128)(4,1)S(1)}, s32[]{:S(2)}) async-start(s8[5242880]{0:T(1024)(128)(4,1)} %bitcast.201), calls=%async_computation.4 | async-start | bytes 8388608 | tf_op jit(solution)/shard_map/while
  343.9 11.7 %slice-start = ((s8[6684672]{0:T(1024)(128)(4,1)}), s8[2490368]{0:T(1024)(128)(4,1)S(1)}, s32[]{:S(2)}) async-start(s8[6684672]{0:T(1024)(128)(4,1)} %bitcast.181), calls=%async_computation.1 | async-start | bytes 4980736 | tf_op jit(solution)/shard_map/while
  347.0 8.6 %slice-start.1 = ((s8[6684672]{0:T(1024)(128)(4,1)}), s8[4194304]{0:T(1024)(128)(4,1)S(1)}, s32[]{:S(2)}) async-start(s8[6684672]{0:T(1024)(128)(4,1)} %bitcast.181), calls=%async_computation.2 | async-start | bytes 8388608 | tf_op jit(solution)/shard_map/while
  357.4 0.7 copy-start.8
  606.3 7.4 %copy-start.2 = (f32[640,640]{1,0:T(8,128)S(1)}, f32[640,640]{1,0:T(8,128)}, u32[]{:S(2)}) copy-start(f32[640,640]{1,0:T(8,128)} %get-tuple-element.757) | copy-start | bytes 4915204
  606.3 7.4 %copy-start.3 = (f32[640,640]{1,0:T(8,128)S(1)}, f32[640,640]{1,0:T(8,128)}, u32[]{:S(2)}) copy-start(f32[640,640]{1,0:T(8,128)} %get-tuple-element.758) | copy-start | bytes 4915204
Sparse Core Ops, SparseCore 0:
  357.6 248.6 all-reduce.8
where the time goes:
time: 649 us; the launch traced here: 640 us
  waiting for transfers between devices  200 us (31%)
  local copies, waits for them, and re-layouts  149 us (23%)
  other arithmetic  109 us (17%)
  matrix products  68.8 us (11%)
  loops' own time  47.9 us (7%)
  blocking collectives  44.8 us (7%)
  between operations  21.2 us (3%)
    psum x1, waiting for transfers between devices, per_device(): lax.psum((grads[0], grads[1], grads[2], grads[3], grads[4]), ('dp', 'rep'))  200 us
    another operation x1, loops' own time, lattice(): lax.scan(both_ways, (first_diag, neg_grid), inputs)  46.1 us
    psum x1, blocking collectives, per_device(): lax.psum((grads[0], grads[1], grads[2], grads[3], grads[4]), ('dp', 'rep'))  44.8 us
    dynamic_slice x256, local copies, waits for them, and re-layouts, lattice(): lax.scan(both_ways, (first_diag, neg_grid), inputs)  39.8 us
    gather x9, local copies, waits for them, and re-layouts, unskewed(): by_utterance[:, frame_ids[:, None] + positions[None, :], positions[None, :]]  30.5 us
    reduce_sum x2, other arithmetic, joint_forward(): jnp.sum(jnp.where(is_target, log_probs, 0.0), axis=1)  25.4 us
    gather x6, local copies, waits for them, and re-layouts, skewed(): grid[:, jnp.clip(frame_index, 0, num_frames - 1), positions[None, :]]  25.2 us
    dynamic_update_slice x6, local copies, waits for them, and re-layouts, local_sums(): lax.scan(forward_one, None, (enc, pred, labels))  24.7 us
  transfers between devices with their start and end apart: 1, of which 1 were waited for; matrix products, arithmetic and copies ran while one was open for 0% of the time, Pallas kernels for 0%

commit v1 on v0

--- a/solution.py
+++ b/solution.py
@@ -202,7 +202,7 @@
     count_local = jnp.sum(label_len).astype(jnp.float32)
     param_count = jnp.float32(w_enc.size + w_pred.size + w_out.size + b_out.size + b_joint.size)
     loss_total, label_total = lax.psum((loss_local, count_local), ("dp", "rep"))
-    summed = lax.psum((grads[0], grads[1], grads[2], grads[3], grads[4]), ("dp", "rep"))
+    summed = lax.psum(lax.psum((grads[0], grads[1], grads[2], grads[3], grads[4]), "rep"), "dp")
     scale = lax.rsqrt(squares(summed) / param_count + EPS)
     result = tuple((item * scale for item in summed))
     return (result[0], result[1], result[2], result[3], result[4], loss_total / label_total)

time: 649 us -> 1080 us (1.66)
  waiting for transfers between devices: 200 us -> 576 us
  blocking collectives: 44.8 us -> 96.2 us
    psum x1 -> x2, waiting for transfers between devices: 200 us -> 576 us  [the longest x1 333 us: per_device(): lax.psum(lax.psum((grads[0], grads[1], grads[2], grads[3], grads[4]), 're...]
    psum x1 -> x3, blocking collectives: 44.8 us -> 96.2 us  [the longest x1 44.4 us: per_device(): loss_total, label_total = lax.psum((loss_local, count_local), ('dp', 'rep'))]
  transfers between devices with their start and end apart: 1 -> 2, of which waited for: 1 -> 2; matrix products, arithmetic and copies ran while one was open for 0% -> 0% of each run, Pallas kernels for 0% -> 0%
where the time goes in v1:
time: 1080 us; the launch traced here: 1070 us
  waiting for transfers between devices  576 us (53%)
  local copies, waits for them, and re-layouts  149 us (14%)
  other arithmetic  109 us (10%)
  blocking collectives  96.2 us (9%)
  matrix products  68.8 us (6%)
  loops' own time  48.1 us (4%)
  between operations  21.3 us (2%)
    psum x1, waiting for transfers between devices, per_device(): lax.psum(lax.psum((grads[0], grads[1], grads[2], grads[3], grads[4]), 're...  333 us
    psum x1, waiting for transfers between devices, per_device(): lax.psum((grads[0], grads[1], grads[2], grads[3], grads[4]), 'rep')  243 us
    another operation x1, loops' own time, lattice(): lax.scan(both_ways, (first_diag, neg_grid), inputs)  46.1 us
    psum x1, blocking collectives, per_device(): loss_total, label_total = lax.psum((loss_local, count_local), ('dp', 'rep'))  44.4 us
    psum x1, blocking collectives, per_device(): lax.psum(lax.psum((grads[0], grads[1], grads[2], grads[3], grads[4]), 're...  40.5 us
    dynamic_slice x256, local copies, waits for them, and re-layouts, lattice(): lax.scan(both_ways, (first_diag, neg_grid), inputs)  39.8 us
    gather x9, local copies, waits for them, and re-layouts, unskewed(): by_utterance[:, frame_ids[:, None] + positions[None, :], positions[None, :]]  30.3 us
    reduce_sum x2, other arithmetic, joint_forward(): jnp.sum(jnp.where(is_target, log_probs, 0.0), axis=1)  25.4 us
  transfers between devices with their start and end apart: 2, of which 2 were waited for; matrix products, arithmetic and copies ran while one was open for 0% of the time, Pallas kernels for 0%

profile of v1, /device:TPU:0, one launch (start us, length us, event | category | flops | bytes accessed | tf_op | source)
XLA Modules:
  0.0 1067.3 jit_solution(571260400173169778)
XLA Ops:
  11.1 88.6 %while.58 = (s32[]{:T(128)}, bf16[2,816,640]{2,1,0:T(8,128)(2,1)}, f32[2,816,4096]{2,1,0:T(8,128)}, f32[2,48,17]{2,1,0:T(8,128)S(1)}, f32[2,48,17]{2,1,0:T(8,128...) while((s32[]{:T(128)}, bf16[2,816,640]{2,1,0:T(8,128)(2,1)}, ...), condition=%wide.region_4.5_spmd, body=%wide.region_0.4_spmd.sunk | while | flops 4369261056 | bytes 147507888 | solution.py:167
  11.9 1.4 convolution_add_fusion.2
  13.3 1.4 fusion.76
  16.4 7.5 add_reduce_fusion.2
  23.9 2.3 exponential_reduce_fusion.2
  26.2 2.5 copy-done.1
  28.9 12.7 %select_reduce_fusion.2 = (f32[816]{0:T(1024)S(1)}, f32[816,4096]{1,0:T(8,128)}) fusion(s32[816]{0:T(1024)S(1)} %eq.178, f32[816]{0:T(1024)S(1)} %log.11, f32[816]{0:T(1024)S(1)} %get-tuple-element.1058, f32[816,4096]{1,0:T(8,128)} %copy-done.1, f32[4096]{0:T(1024)S(1)} %convert_element_type.65), kind=kLoop, calls=%fused_computation.62.clone.1 | loop fusion | flops 20053200 | bytes 26768128 | tf_op jit(solution)/shard_map/while/body/eval_jaxpr/reduce_sum | solution.py:110
  41.6 1.2 slice_reduce_fusion.2
  43.1 11.3 %bitcast_dynamic-update-slice_fusion.5 = f32[2,816,4096]{2,1,0:T(8,128)} fusion(f32[2,816,4096]{2,1,0:T(8,128)} %get-tuple-element.1125, s32[]{:T(128)} %get-tuple-element.1123, f32[816,4096]{1,0:T(8,128)} %get-tuple-element.1059), kind=kLoop, calls=%fused_computation.61.clone.1 | loop fusion | bytes 26739200 | tf_op jit(solution)/shard_map/while/body/jit(dynamic_update_index_in_dim)/dynamic_update_slice | solution.py:167
  56.1 1.4 convolution_add_fusion.2
  57.5 1.4 fusion.76
  60.6 7.5 add_reduce_fusion.2
  68.1 2.3 exponential_reduce_fusion.2
  70.5 2.5 copy-done.1
  73.2 12.7 %select_reduce_fusion.2 = (f32[816]{0:T(1024)S(1)}, f32[816,4096]{1,0:T(8,128)}) fusion(s32[816]{0:T(1024)S(1)} %eq.178, f32[816]{0:T(1024)S(1)} %log.11, f32[816]{0:T(1024)S(1)} %get-tuple-element.1058, f32[816,4096]{1,0:T(8,128)} %copy-done.1, f32[4096]{0:T(1024)S(1)} %convert_element_type.65), kind=kLoop, calls=%fused_computation.62.clone.1 | loop fusion | flops 20053200 | bytes 26768128 | tf_op jit(solution)/shard_map/while/body/eval_jaxpr/reduce_sum | solution.py:110
  85.9 1.2 slice_reduce_fusion.2
  87.3 11.3 %bitcast_dynamic-update-slice_fusion.5 = f32[2,816,4096]{2,1,0:T(8,128)} fusion(f32[2,816,4096]{2,1,0:T(8,128)} %get-tuple-element.1125, s32[]{:T(128)} %get-tuple-element.1123, f32[816,4096]{1,0:T(8,128)} %get-tuple-element.1059), kind=kLoop, calls=%fused_computation.61.clone.1 | loop fusion | bytes 26739200 | tf_op jit(solution)/shard_map/while/body/jit(dynamic_update_index_in_dim)/dynamic_update_slice | solution.py:167
  100.8 12.3 %gather_fusion = f32[1088,2]{1,0:T(8,128)S(1)} fusion(f32[2,48,17]{0,1,2:T(8,128)S(1)} %copy.55, s32[1088]{0:T(1024)S(1)} %reshape.180), kind=kCustom, calls=%fused_computation | custom fusion | bytes 26112 | tf_op jit(solution)/shard_map/gather | solution.py:21
  113.6 12.1 %gather_fusion.1 = f32[1088,2]{1,0:T(8,128)S(1)} fusion(f32[2,48,17]{0,1,2:T(8,128)S(1)} %copy.57, s32[1088]{0:T(1024)S(1)} %reshape.180), kind=kCustom, calls=%fused_computation.1 | custom fusion | bytes 26112 | tf_op jit(solution)/shard_map/gather | solution.py:21
  126.3 106.5 %while.59 = (s32[]{:T(128)}, f32[2,17]{1,0:T(2,128)S(1)}, f32[2,17]{1,0:T(2,128)S(1)}, f32[64,2,17]{2,1,0:T(2,128)S(1)}, f32[64,2,17]{2,1,0:T(2,128)S(1)}, /*ind...) while((s32[]{:T(128)}, f32[2,17]{1,0:T(2,128)S(1)}, ...), condition=%wide.region_6.7_spmd.clone, body=%wide.region_5.6_spmd.clone.sunk | while | flops 1434 | bytes 22799 | solution.py:84
  233.9 9.8 gather_fusion.2
  245.2 9.8 gather_fusion.4
  256.0 9.8 gather_fusion.3
  266.2 91.1 %while.60 = (s32[]{:T(128)}, f32[]{:T(128)}, f32[640,640]{1,0:T(8,128)}, f32[640,640]{1,0:T(8,128)}, f32[640,4096]{1,0:T(8,128)}, /*index=5*/f32[4096]{0:T(1024)...) while((s32[]{:T(128)}, f32[]{:T(128)}, ...), condition=%wide.region_12.13_spmd.clone, body=%wide.region_7.12_spmd.clone.sunk | while | flops 8649718784 | bytes 146314000 | solution.py:183
  269.0 11.2 %fusion.89 = bf16[816,4096]{1,0:T(8,128)(2,1)} fusion(f32[2,816,4096]{2,1,0:T(8,128)} %get-tuple-element.1264, s32[]{:T(128)} %get-tuple-element.1234, f32[816]{0:T(1024)S(1)} %reshape.215, s32[816]{0:T(1024)S(1)} %eq.189, f32[816]{0:T(1024)S(1)} %exp.63, f32[816]{0:T(1024)S(1)} %add.414, pred[4096]{0:T(1024)(128)(4,1)S(1)} %iota_compare_fusion.4), kind=kLoop, calls=%fused_computation.33.clone.1 | loop fusion | flops 23396352 | bytes 20071172 | tf_op jit(solution)/shard_map/while/body/eval_jaxpr/convert_element_type | solution.py:134
  280.2 10.6 select_add_fusion.12
  290.8 8.1 subtract_multiply_fusion.2
  299.0 3.1 reshape.216
  302.1 2.5 fusion.90
  304.6 1.6 select_add_fusion.11
  306.2 1.6 select_add_fusion.10
  307.8 1.1 convert_reduce_fusion.4
  312.2 11.2 %fusion.89 = bf16[816,4096]{1,0:T(8,128)(2,1)} fusion(f32[2,816,4096]{2,1,0:T(8,128)} %get-tuple-element.1264, s32[]{:T(128)} %get-tuple-element.1234, f32[816]{0:T(1024)S(1)} %reshape.215, s32[816]{0:T(1024)S(1)} %eq.189, f32[816]{0:T(1024)S(1)} %exp.63, f32[816]{0:T(1024)S(1)} %add.414, pred[4096]{0:T(1024)(128)(4,1)S(1)} %iota_compare_fusion.4), kind=kLoop, calls=%fused_computation.33.clone.1 | loop fusion | flops 23396352 | bytes 20071172 | tf_op jit(solution)/shard_map/while/body/eval_jaxpr/convert_element_type | solution.py:134
  323.4 12.1 %select_add_fusion.12 = f32[640,4096]{1,0:T(8,128)} fusion(f32[640,4096]{1,0:T(8,128)} %get-tuple-element.1238, bf16[816,4096]{1,0:T(8,128)(2,1)} %fusion.89, pred[]{:T(512)S(6)} %compare.12, bf16[2,816,640]{2,1,0:T(8,128)(2,1)} %get-tuple-element.1271, s32[]{:T(128)} %get-tuple-element.1234), kind=kOutput, calls=%fused_computation.36.clone.1 | convolution fusion | flops 4283432960 | bytes 28701184 | tf_op jit(solution)/shard_map/while/body/eval_jaxpr/dot_general | solution.py:135
  335.8 8.1 subtract_multiply_fusion.2
  343.9 3.1 reshape.216
  347.0 2.5 fusion.90
  349.5 3.0 select_add_fusion.11
  352.5 3.0 select_add_fusion.10
  357.5 242.6 %all-reduce.15.cloned.1.call-done = (f32[640,640]{1,0:T(8,128)}, f32[640,640]{1,0:T(8,128)}, f32[640,4096]{1,0:T(8,128)}) async-done(((f32[640,640]{1,0:T(8,128)}, f32[640,640]{1,0:T(8,128)}, f32[640,4096]{1,0:T(8,128)}), (f32[640,640]{1,0:T(8,128)}, f32[640,640]{1,0:T(8,128)}, f32[640,4096]{1,0:T(8,128)})) %all-reduce.15.cloned.1.call-update) | async-done | bytes 13762576 | tf_op jit(solution)/shard_map/psum | solution.py:205
  602.0 44.4 %all-reduce.5 = (f32[]{:T(128)}, f32[]{:T(128)}) all-reduce(f32[]{:T(128)} %get-tuple-element.408, f32[]{:T(128)S(6)} %convert_element_type.42), channel_id=1, replica_groups=mesh['dp'=8,'rep'=4] {'dp','rep'}, use_global_device_ids=true, to_apply=%region_28.29 | all-reduce | flops 2 | bytes 16 | tf_op jit(solution)/shard_map/psum | solution.py:204
  647.8 11.3 %all-reduce.8 = (f32[4096]{0:T(1024)S(1)}, f32[640]{0:T(1024)S(1)}) all-reduce(f32[4096]{0:T(1024)S(1)} %get-tuple-element.406, f32[640]{0:T(1024)S(1)} %get-tuple-element.407), channel_id=1, replica_groups=mesh['dp'=8,'rep'=4] {'rep'}, use_global_device_ids=true, to_apply=%region_22.23 | all-reduce | flops 4736 | bytes 37888 | tf_op jit(solution)/shard_map/psum | solution.py:205
  659.1 40.5 %all-reduce.6 = (f32[4096]{0:T(1024)S(1)}, f32[640]{0:T(1024)S(1)}) all-reduce(f32[4096]{0:T(1024)S(1)} %get-tuple-element.760, f32[640]{0:T(1024)S(1)} %get-tuple-element.761), channel_id=1, replica_groups=mesh['dp'=8,'rep'=4] {'dp'}, use_global_device_ids=true, to_apply=%region_23.24 | all-reduce | flops 4736 | bytes 37888 | tf_op jit(solution)/shard_map/psum | solution.py:205
  700.7 333.0 %all-reduce.13.cloned.1.call-done = (f32[640,640]{1,0:T(8,128)}, f32[640,640]{1,0:T(8,128)}, f32[640,4096]{1,0:T(8,128)}) async-done(((f32[640,640]{1,0:T(8,128)}, f32[640,640]{1,0:T(8,128)}, f32[640,4096]{1,0:T(8,128)}), (f32[640,640]{1,0:T(8,128)}, f32[640,640]{1,0:T(8,128)}, f32[640,4096]{1,0:T(8,128)})) %all-reduce.13.cloned.1.call-update) | async-done | bytes 13762576 | tf_op jit(solution)/shard_map/psum | solution.py:205
  1033.7 7.4 multiply_reduce_fusion
  1046.6 9.7 broadcast_multiply_fusion
  1056.3 1.3 broadcast_multiply_fusion.1
  1057.6 1.3 broadcast_multiply_fusion.2
  (954 shorter events, 89.2 us)
Async XLA Ops:
  7.2 592.9 %all-reduce.15.cloned.1.call-start = ((), (), s32[]{:S(2)}) async-start(), calls=%async_computation.1 | async-start | bytes 27525120 | tf_op jit(solution)/shard_map/psum | solution.py:205
  11.0 89.7 %copy-start.5 = (s32[64,17,1]{1,0,2:T(8,128)S(1)}, s32[64,17,1]{1,0,2:T(8,128)}, u32[]{:S(2)}) copy-start(s32[64,17,1]{1,0,2:T(8,128)} %fusion.34) | copy-start | bytes 13060
  11.0 115.0 %copy-start.14 = (pred[64,17]{1,0:T(8,128)(4,1)S(1)}, pred[64,17]{1,0:T(8,128)(4,1)}, u32[]{:S(2)}) copy-start(pred[64,17]{1,0:T(8,128)(4,1)} %compare_and_fusion) | copy-start | bytes 3268
  11.0 115.1 %copy-start.6 = (s32[64,17]{1,0:T(8,128)S(1)}, s32[64,17]{1,0:T(8,128)}, u32[]{:S(2)}) copy-start(s32[64,17]{1,0:T(8,128)} %iota_subtract_fusion) | copy-start | bytes 13060
  11.0 115.2 %copy-start.16 = (f32[17]{0:T(128)S(1)}, f32[17]{0:T(128)}, u32[]{:S(2)}) copy-start(f32[17]{0:T(128)} %compare_select_fusion.7) | copy-start | bytes 208
  11.1 115.2 %copy-start.7 = (s32[2]{0:T(128)S(1)}, s32[2]{0:T(128)}, u32[]{:S(2)}) copy-start(s32[2]{0:T(128)} %param.20) | copy-start | bytes 28
  11.1 115.2 %copy-start.10 = (f32[64,2,17]{2,1,0:T(2,128)S(1)}, f32[64,2,17]{2,1,0:T(2,128)}, u32[]{:S(2)}) copy-start(f32[64,2,17]{2,1,0:T(2,128)} %custom-call.20) | copy-start | bytes 26116
  11.1 115.2 %copy-start.11 = (f32[64,2,17]{2,1,0:T(2,128)S(1)}, f32[64,2,17]{2,1,0:T(2,128)}, u32[]{:S(2)}) copy-start(f32[64,2,17]{2,1,0:T(2,128)} %custom-call.21) | copy-start | bytes 26116
  11.1 115.2 %copy-start.12 = (f32[64,2,17]{2,1,0:T(2,128)S(1)}, f32[64,2,17]{2,1,0:T(2,128)}, u32[]{:S(2)}) copy-start(f32[64,2,17]{2,1,0:T(2,128)} %custom-call.22) | copy-start | bytes 26116
  11.1 115.2 %copy-start.13 = (s32[2]{0:T(128)S(1)}, s32[2]{0:T(128)}, u32[]{:S(2)}) copy-start(s32[2]{0:T(128)} %param.19) | copy-start | bytes 28
  11.1 115.2 %copy-start.15 = (f32[2,17]{1,0:T(2,128)S(1)}, f32[2,17]{1,0:T(2,128)}, u32[]{:S(2)}) copy-start(f32[2,17]{1,0:T(2,128)} %custom-call.10) | copy-start | bytes 412
  23.9 4.8 copy-start.1
  23.9 4.8 copy-start.17
  68.1 4.8 copy-start.1
  68.1 4.8 copy-start.17
  99.7 134.1 %copy-start.9 = (s32[48,17,1]{1,0,2:T(8,128)S(1)}, s32[48,17,1]{1,0,2:T(8,128)}, u32[]{:S(2)}) copy-start(s32[48,17,1]{1,0,2:T(8,128)} %fusion.37) | copy-start | bytes 9796
  113.2 153.1 %copy-start.4 = (bf16[2,48,640]{2,1,0:T(8,128)(2,1)S(1)}, bf16[2,48,640]{2,1,0:T(8,128)(2,1)}, u32[]{:S(2)}) copy-start(bf16[2,48,640]{2,1,0:T(8,128)(2,1)} %get-tuple-element.1299) | copy-start | bytes 368644
  113.2 153.1 %copy-start.18 = (s32[2,16]{1,0:T(2,128)S(1)}, s32[2,16]{1,0:T(2,128)}, u32[]{:S(2)}) copy-start(s32[2,16]{1,0:T(2,128)} %get-tuple-element.1307) | copy-start | bytes 388
  269.0 21.8 %slice-start.2 = ((s8[5242880]{0:T(1024)(128)(4,1)}), s8[1048576]{0:T(1024)(128)(4,1)S(1)}, s32[]{:S(2)}) async-start(s8[5242880]{0:T(1024)(128)(4,1)} %bitcast.201), calls=%async_computation.4 | async-start | bytes 2097152 | tf_op jit(solution)/shard_map/while
  280.2 10.6 copy-start
  280.2 10.6 slice-start.3
  299.0 8.8 slice-start
  302.1 5.7 slice-start.1
  312.2 23.3 %slice-start.2 = ((s8[5242880]{0:T(1024)(128)(4,1)}), s8[1048576]{0:T(1024)(128)(4,1)S(1)}, s32[]{:S(2)}) async-start(s8[5242880]{0:T(1024)(128)(4,1)} %bitcast.201), calls=%async_computation.4 | async-start | bytes 2097152 | tf_op jit(solution)/shard_map/while
  323.4 12.1 %copy-start = (bf16[816,4096]{1,0:T(8,128)(2,1)S(1)}, bf16[816,4096]{1,0:T(8,128)(2,1)}, u32[]{:S(2)}) copy-start(bf16[816,4096]{1,0:T(8,128)(2,1)} %fusion.89) | copy-start | bytes 20054020 | tf_op jit(solution)/shard_map/while
  323.4 12.4 %slice-start.3 = ((s8[5242880]{0:T(1024)(128)(4,1)}), s8[4194304]{0:T(1024)(128)(4,1)S(1)}, s32[]{:S(2)}) async-start(s8[5242880]{0:T(1024)(128)(4,1)} %bitcast.201), calls=%async_computation.5 | async-start | bytes 8388608 | tf_op jit(solution)/shard_map/while
  343.9 11.7 %slice-start = ((s8[6684672]{0:T(1024)(128)(4,1)}), s8[2490368]{0:T(1024)(128)(4,1)S(1)}, s32[]{:S(2)}) async-start(s8[6684672]{0:T(1024)(128)(4,1)} %bitcast.181), calls=%async_computation.2 | async-start | bytes 4980736 | tf_op jit(solution)/shard_map/while
  347.0 8.6 slice-start.1
  357.4 676.3 %all-reduce.13.cloned.1.call-start = ((), (), s32[]{:S(2)}) async-start(), calls=%async_computation | async-start | bytes 27525120 | tf_op jit(solution)/shard_map/psum | solution.py:205
  600.1 0.7 copy-start.8
  1033.7 7.4 copy-start.2
  1033.7 7.4 copy-start.3
Sparse Core Ops, SparseCore 0:
  357.5 242.4 all-reduce.14
  604.8 428.8 all-reduce.12
